TPU v7x, 128 devices: a whole 4x4x4 slice. The times are simulated.
128 devices in a mesh: row: 16 (over y_hi, z, core), col: 8 (over y_lo, x).
Axes of the slice: x: 4, y: 4 (y_hi: 2, y_lo: 2; y = y_hi * 2 + y_lo), z: 4, core: 2. Of those that a mesh axis runs over, the one named last changes fastest.
Arguments:
- pair: bfloat16 [1024, 1024, 128], P('row', 'col'), may hold values from -6 to 6
- relpos: bfloat16 [128, 128], replicated, may hold values from -4 to 4
- pair_gain: float32 [128], replicated, may hold values from 0.1 to 1.9
- bias_weight: bfloat16 [128, 12], replicated, may hold values from -0.5 to 0.5
- single: float32 [1024, 384], P(('row', 'col')), may hold values from -6 to 6
- rotation_params: float32 [3, 1024], P(None, ('row', 'col')), may hold values from -4 to 4
- translation: float32 [3, 1024], P(None, ('row', 'col')), may hold values from -9 to 9
- residue_index: int32 [1024], P(('row', 'col')), may hold values from 0 to 203776, as said below
- residue_mask: int32 [1024], P(('row', 'col')), may hold values 0 or 1
- w_scalar: float32 [384, 576], replicated, may hold values from -0.3125 to 0.3125
- w_points: float32 [384, 576], replicated, may hold values from -0.3125 to 0.3125
- head_weights: float32 [12], replicated, may hold values from -2 to 1.5
- w_out: float32 [2112, 384], replicated, may hold values from -0.125 to 0.125
- w_hidden: float32 [384, 384], replicated, may hold values from -0.3125 to 0.3125
- w_back: float32 [384, 384], replicated, may hold values from -0.3125 to 0.3125
- w_frame: float32 [384, 6], replicated, may hold values from -0.078125 to 0.078125
Outputs:
- single_out: float32 [1024, 384], P(('row', 'col'))
- frames: float32 [12, 1024], P(None, ('row', 'col'))
Inputs may be any that keep to these rules, and one draw needn't show every extreme that they name: residue_index is strictly increasing along the crop, begins at 0 and ends at exactly 203776.
All inputs are finite; a program needn't handle non-finite values. No bound on the sum of `residue_mask` on one device may be relied on, other than what follows from the above.
Results may differ from a plain program's by a relative error of at most 0.0025.
Values may be sent and summed in bfloat16 or wider, within the bound.
A program may use at most 64 MiB of HBM per device.

v0:
```python
import math
import jax
import jax.numpy as jnp
from jax import lax
from jax.sharding import PartitionSpec as P

H = 12
C = 16
PQ = 4
PV = 8
BINS = 128
ITERS = 3
NORM_EPSILON = 1e-05
MASKED_LOGIT = -100000.0
NORM_FLOOR = 0.1
HIGHEST_PRECISION = lax.Precision.HIGHEST


def rows_first(arrays, axis, dims):
    turned = [jnp.moveaxis(a, dim, 0) for a, dim in zip(arrays, dims)]
    both = jnp.concatenate([t.reshape(len(t), -1) for t in turned], axis=1)
    whole, at, outs = (lax.all_gather(both, axis, axis=0, tiled=True), 0, [])
    for t, dim in zip(turned, dims):
        piece = whole[:, at : at + t[0].size].reshape(-1, *t.shape[1:])
        outs.append(jnp.moveaxis(piece, 0, dim))
        at += t[0].size
    return tuple(outs)


def in_order(parts, dim):
    shape = list(parts.shape[1:])
    shape[dim] *= parts.shape[0]
    return jnp.moveaxis(parts, 0, dim).reshape(shape)


def copy_for_each(value, axis):
    copies = jnp.broadcast_to(value, (lax.axis_size(axis), *value.shape))
    return lax.all_to_all(copies, axis, split_axis=0, concat_axis=0, tiled=True)


def gather_directly(value, axis, dim):
    return in_order(copy_for_each(value, axis), dim)


def broadcast(value, axis, root):
    return lax.dynamic_index_in_dim(lax.all_gather(value, axis), root, 0, keepdims=False)


def of_everyone(value, axis):
    return copy_for_each(value, axis).max(axis=0)


def sent_together(arrays, axis, dim, along):
    both = jnp.concatenate(arrays, axis=along)
    whole, at, outs = (lax.psum_scatter(both, axis, scatter_dimension=dim, tiled=True), 0, [])
    for a in arrays:
        outs.append(lax.slice_in_dim(whole, at, at + a.shape[along], axis=along))
        at += a.shape[along]
    return tuple(outs)


def layer_norm(values):
    center = values - jnp.mean(values, axis=-1, keepdims=True)
    spread = jnp.mean(center * center, axis=-1, keepdims=True)
    return center * lax.rsqrt(spread + NORM_EPSILON)


def rotation_from(update):
    quat_b, quat_c, quat_d = (update[0], update[1], update[2])
    inverse = 1.0 / (1.0 + quat_b * quat_b + quat_c * quat_c + quat_d * quat_d)
    entries = [
        1.0 + quat_b * quat_b - quat_c * quat_c - quat_d * quat_d,
        2.0 * (quat_b * quat_c - quat_d),
        2.0 * (quat_b * quat_d + quat_c),
        2.0 * (quat_b * quat_c + quat_d),
        1.0 - quat_b * quat_b + quat_c * quat_c - quat_d * quat_d,
        2.0 * (quat_c * quat_d - quat_b),
        2.0 * (quat_b * quat_d - quat_c),
        2.0 * (quat_c * quat_d + quat_b),
        1.0 - quat_b * quat_b - quat_c * quat_c + quat_d * quat_d,
    ]
    return jnp.stack(entries) * inverse


def to_global(rotation, points, translation):
    return jnp.stack(
        [
            rotation[3 * component] * points[0]
            + rotation[3 * component + 1] * points[1]
            + rotation[3 * component + 2] * points[2]
            + translation[component]
            for component in range(3)
        ]
    )


def to_local(rotation, points, translation):
    moved = [points[component] - translation[component] for component in range(3)]
    return jnp.stack(
        [
            rotation[component] * moved[0]
            + rotation[3 + component] * moved[1]
            + rotation[6 + component] * moved[2]
            for component in range(3)
        ]
    )


def compose(rotation, translation, update):
    turn = rotation_from(update[:3])
    new_rotation = jnp.stack(
        [
            rotation[3 * left] * turn[right]
            + rotation[3 * left + 1] * turn[3 + right]
            + rotation[3 * left + 2] * turn[6 + right]
            for left in range(3)
            for right in range(3)
        ]
    )
    new_translation = jnp.stack(
        [
            rotation[3 * left] * update[3]
            + rotation[3 * left + 1] * update[4]
            + rotation[3 * left + 2] * update[5]
            + translation[left]
            for left in range(3)
        ]
    )
    return (new_rotation, new_translation)


def project(single, rotation, translation, w_scalar, w_points):
    count = single.shape[0]
    scalars = jnp.dot(
        single, w_scalar, precision=HIGHEST_PRECISION, preferred_element_type=jnp.float32
    ).T
    scalars = scalars.reshape(3, H * C, count).astype(jnp.bfloat16)
    points = jnp.dot(
        single, w_points, precision=HIGHEST_PRECISION, preferred_element_type=jnp.float32
    ).T
    query_local = points[: 3 * H * PQ].reshape(3, H * PQ, count)
    key_local = points[3 * H * PQ : 6 * H * PQ].reshape(3, H * PQ, count)
    value_local = points[6 * H * PQ :].reshape(3, H * PV, count)
    return (
        scalars,
        to_global(rotation, query_local, translation),
        to_global(rotation, key_local, translation),
        to_global(rotation, value_local, translation),
    )


def advance(
    single, rotation, translation, scalar_out, point_out, pair_out, w_out, w_hidden, w_back, w_frame
):
    count = single.shape[0]
    local = to_local(rotation, point_out, translation)
    lengths = jnp.sqrt(jnp.sum(local * local, axis=0) + NORM_FLOOR)
    features = jnp.concatenate(
        [scalar_out, local.reshape(3 * H * PV, count), lengths, pair_out], axis=0
    )
    mixed = jnp.dot(
        features.T, w_out, precision=HIGHEST_PRECISION, preferred_element_type=jnp.float32
    )
    single = layer_norm(single + mixed)
    hidden = jax.nn.relu(
        jnp.dot(single, w_hidden, precision=HIGHEST_PRECISION, preferred_element_type=jnp.float32)
    )
    single = layer_norm(
        single
        + jnp.dot(hidden, w_back, precision=HIGHEST_PRECISION, preferred_element_type=jnp.float32)
    )
    update = jnp.dot(
        single, w_frame, precision=HIGHEST_PRECISION, preferred_element_type=jnp.float32
    ).T
    rotation, translation = compose(rotation, translation, update)
    return (single, rotation, translation)


def attend_block(
    query, keyval, query_side, key_side, value_side, bias, normed, pair_live, point_scale
):
    heads_query = query.reshape(H, C, -1)
    keys = keyval[0].reshape(H, C, -1)
    values = keyval[1].reshape(H, C, -1)
    query_grid = query_side.reshape(3, H, PQ, -1)
    key_grid = key_side.reshape(3, H, PQ, -1)
    value_grid = value_side.reshape(3, H, PV, -1)
    scores = jnp.einsum(
        "hci,hcj->hij", heads_query, keys, preferred_element_type=jnp.float32
    ) / math.sqrt(C)
    cross = jnp.einsum("ahpi,ahpj->hij", query_grid, key_grid, precision=HIGHEST_PRECISION)
    distance = (
        jnp.sum(query_grid * query_grid, axis=(0, 2))[:, :, None]
        + jnp.sum(key_grid * key_grid, axis=(0, 2))[:, None, :]
        - 2.0 * cross
    )
    logits = math.sqrt(1.0 / 3.0) * (scores + bias - point_scale[:, None, None] * distance)
    logits = jnp.where(pair_live[None], logits, MASKED_LOGIT)
    local_max = jnp.max(logits, axis=-1)
    unscaled = jnp.exp(logits - local_max[:, :, None])
    total_weight = jnp.sum(unscaled, axis=-1)
    rounded = unscaled.astype(jnp.bfloat16)
    scalar_sum = jnp.einsum("hij,hcj->hci", rounded, values, preferred_element_type=jnp.float32)
    point_sum = jnp.einsum("hij,ahpj->ahpi", unscaled, value_grid, precision=HIGHEST_PRECISION)
    pair_sum = jnp.einsum("hij,ijc->hci", rounded, normed, preferred_element_type=jnp.float32)
    return (local_max, total_weight, scalar_sum, point_sum, pair_sum)


def body(
    pair,
    relpos,
    pair_gain,
    bias_weight,
    single,
    rotation_params,
    translation,
    residue_index,
    residue_mask,
    w_scalar,
    w_points,
    head_weights,
    w_out,
    w_hidden,
    w_back,
    w_frame,
):
    row_rows = pair.shape[0]
    col_rows = pair.shape[1]
    owned = single.shape[0]
    row_place = lax.axis_index("row")
    col_place = lax.axis_index("col")
    index_all, mask_all = rows_first((residue_index, residue_mask), ("row", "col"), (0, 0))
    query_index = lax.dynamic_slice_in_dim(index_all, row_place * row_rows, row_rows, 0)
    key_index = lax.dynamic_slice_in_dim(index_all, col_place * col_rows, col_rows, 0)
    query_live = lax.dynamic_slice_in_dim(mask_all, row_place * row_rows, row_rows, 0) == 1
    key_live = lax.dynamic_slice_in_dim(mask_all, col_place * col_rows, col_rows, 0) == 1
    pair_live = query_live[:, None] & key_live[None, :]
    span_rows = math.gcd(row_rows, 64)

    def prepare(index):
        offset = (
            jnp.clip(key_index[None, :] - query_index[:, None], -(BINS // 2), BINS // 2 - 1)
            + BINS // 2
        )
        onehot = (offset[:, :, None] == lax.broadcasted_iota(jnp.int32, (1, 1, BINS), 2)).astype(
            jnp.bfloat16
        )
        embedded = jnp.dot(
            onehot.reshape(span_rows * col_rows, BINS), relpos, preferred_element_type=jnp.float32
        )
        summed = pair.astype(jnp.float32) + embedded.reshape(span_rows, col_rows, -1)
        normed_part = (layer_norm(summed) * pair_gain).astype(jnp.bfloat16)
        bias_part = jnp.einsum(
            "ijc,ch->hij", normed_part, bias_weight, preferred_element_type=jnp.float32
        )
        return (normed_part, bias_part)

    normed_blocks, bias_blocks = lax.map(
        prepare, jnp.arange(row_rows // span_rows, dtype=jnp.int32)
    )
    normed = normed_blocks.reshape(row_rows, col_rows, -1)
    bias = bias_blocks.transpose(1, 0, 2, 3).reshape(H, row_rows, col_rows)
    point_scale = jax.nn.softplus(head_weights) * (math.sqrt(2.0 / (9.0 * PQ)) / 2.0)
    rotation = rotation_from(rotation_params)
    state = single
    for step in range(ITERS):
        scalars, query_points, key_points, value_points = project(
            state, rotation, translation, w_scalar, w_points
        )
        query_flat = query_points.reshape(-1, owned)
        key_flat = key_points.reshape(-1, owned)
        value_flat = value_points.reshape(-1, owned)
        block_scalar = gather_directly(scalars, "col", 2)
        block_point = rows_first((query_flat, key_flat, value_flat), "col", (1, 1, 1))
        query = block_scalar[0]
        query_side = block_point[0]
        ratio = lax.axis_size("row") // lax.axis_size("col")
        scalar_pieces = []
        key_pieces = []
        value_pieces = []
        for part in range(ratio):
            root = col_place * ratio + part
            scalar_pieces.append(broadcast(block_scalar[1:], "row", root))
            key_piece, value_piece = (
                broadcast(block_point[1], "row", root),
                broadcast(block_point[2], "row", root),
            )
            key_pieces.append(key_piece)
            value_pieces.append(value_piece)
        keyval = jnp.concatenate(scalar_pieces, axis=2)
        key_side = jnp.concatenate(key_pieces, axis=1)
        value_side = jnp.concatenate(value_pieces, axis=1)
        local_max, total_weight, scalar_sum, point_sum, pair_sum = attend_block(
            query, keyval, query_side, key_side, value_side, bias, normed, pair_live, point_scale
        )
        pair_out = None
        row_top = of_everyone(local_max, "col")
        factor = jnp.exp(local_max - row_top)
        shares = sent_together(
            (
                total_weight * factor,
                (scalar_sum * factor[:, None, :]).reshape(H * C, row_rows),
                (point_sum * factor[None, :, None, :]).reshape(3 * H * PV, row_rows),
                (pair_sum * factor[:, None, :]).reshape(-1, row_rows),
            ),
            "col",
            1,
            0,
        )
        total = shares[0]
        scalar_out = (shares[1].reshape(H, C, owned) / total[:, None, :]).reshape(H * C, owned)
        point_out = (shares[2].reshape(3, H, PV, owned) / total[None, :, None, :]).reshape(
            3, H * PV, owned
        )
        pair_out = (shares[3].reshape(H, -1, owned) / total[:, None, :]).reshape(-1, owned)
        state, rotation, translation = advance(
            state,
            rotation,
            translation,
            scalar_out,
            point_out,
            pair_out,
            w_out,
            w_hidden,
            w_back,
            w_frame,
        )
    frames = jnp.concatenate([rotation, translation], axis=0)
    return (state, frames)


def solution(mesh):
    placed = (
        P("row", "col", None),
        P(),
        P(),
        P(),
        P(("row", "col"), None),
        P(None, ("row", "col")),
        P(None, ("row", "col")),
        P(("row", "col")),
        P(("row", "col")),
        P(),
        P(),
        P(),
        P(),
        P(),
        P(),
        P(),
    )
    return jax.shard_map(
        body,
        mesh=mesh,
        in_specs=placed,
        out_specs=(P(("row", "col"), None), P(None, ("row", "col"))),
        check_vma=False,
    )
```

profile of v0, /device:TPU:0, one launch (start us, length us, event | category | flops | bytes accessed | tf_op | source)
XLA Modules:
  0.0 859.4 jit_solution(4518014439812937433)
XLA Ops:
  10.1 5.4 all-to-all-start
  21.4 29.0 %all_gather.87 = f32[64,576]{1,0:T(8,128)S(1)} all-gather(f32[8,576]{1,0:T(8,128)S(1)} %pad_maximum_fusion.9), channel_id=1, replica_groups=mesh['row'=16,'col'=8] {'col'}, dimensions={0}, use_global_device_ids=true | all-gather | bytes 165888 | tf_op jit(solution)/shard_map/all_gather | solution.py:22
  51.9 311.7 %all-gather.6 = s32[128,8,2]{1,2,0:T(2,128)S(1)} all-gather(s32[1,8,2]{1,2,0:T(2,128)S(1)} %add_bitcast_fusion.27), channel_id=1, replica_groups=mesh['row'=16,'col'=8] {'row','col'}, dimensions={0}, use_global_device_ids=true | all-gather | bytes 8256 | tf_op jit(solution)/shard_map/all_gather | solution.py:22
  363.9 4.1 copy.370
  368.1 3.8 fusion.95
  375.8 24.2 %all-gather.7 = f32[16,144,64]{1,2,0:T(8,128)} all-gather(f32[1,144,64]{1,2,0:T(8,128)} %get-tuple-element.84), channel_id=2, replica_groups=mesh['row'=16,'col'=8] {'row'}, dimensions={0}, use_global_device_ids=true | all-gather | bytes 626688 | tf_op jit(solution)/shard_map/all_gather | solution.py:46
  405.2 3.2 multiply_convert_fusion
  413.5 23.1 %all_gather.86 = bf16[16,2,192,64]{2,3,1,0:T(8,128)(2,1)S(1)} all-gather(bf16[1,2,192,64]{2,3,1,0:T(8,128)(2,1)S(1)} %slice_bitcast_fusion.11), channel_id=1, replica_groups=mesh['row'=16,'col'=8] {'row'}, dimensions={0}, use_global_device_ids=true | all-gather | bytes 835584 | tf_op jit(solution)/shard_map/all_gather | solution.py:46
  443.1 3.3 all-to-all-start.1
  449.5 3.0 all-to-all-done.1
  457.0 2.8 fusion.2
  467.6 33.0 %reduce-scatter.4.cloned.1.call-done = f32[2028,8]{0,1:T(8,128)} async-done(((f32[2028,64]{0,1:T(8,128)}), f32[2028,8]{0,1:T(8,128)}) %reduce-scatter.4.cloned.1.call-update) | async-done | bytes 64912 | tf_op jit(solution)/shard_map/reduce_scatter | solution.py:55
  511.3 28.2 %all_gather.94 = f32[64,576]{1,0:T(8,128)S(1)} all-gather(f32[8,576]{1,0:T(8,128)S(1)} %pad_maximum_fusion.10), channel_id=1, replica_groups=mesh['row'=16,'col'=8] {'col'}, dimensions={0}, use_global_device_ids=true | all-gather | bytes 165888 | tf_op jit(solution)/shard_map/all_gather | solution.py:22
  541.7 3.4 all-to-all-start.2
  546.1 26.9 %all-gather.9 = f32[16,144,64]{1,2,0:T(8,128)S(1)} all-gather(f32[1,144,64]{1,2,0:T(8,128)S(1)} %get-tuple-element.82), channel_id=4, replica_groups=mesh['row'=16,'col'=8] {'row'}, dimensions={0}, use_global_device_ids=true | all-gather | bytes 626688 | tf_op jit(solution)/shard_map/all_gather | solution.py:46
  578.5 22.4 %all_gather.93 = bf16[16,2,192,64]{2,3,1,0:T(8,128)(2,1)S(1)} all-gather(bf16[1,2,192,64]{2,3,1,0:T(8,128)(2,1)S(1)} %slice_bitcast_fusion.8), channel_id=1, replica_groups=mesh['row'=16,'col'=8] {'row'}, dimensions={0}, use_global_device_ids=true | all-gather | bytes 835584 | tf_op jit(solution)/shard_map/all_gather | solution.py:46
  607.2 5.2 all-to-all-start.3
  635.1 35.0 %reduce-scatter.6.cloned.1.call-done = f32[2028,8]{0,1:T(8,128)} async-done(((f32[2028,64]{0,1:T(8,128)}), f32[2028,8]{0,1:T(8,128)}) %reduce-scatter.6.cloned.1.call-update) | async-done | bytes 64912 | tf_op jit(solution)/shard_map/reduce_scatter | solution.py:55
  682.4 28.2 %all_gather.101 = f32[64,576]{1,0:T(8,128)S(1)} all-gather(f32[8,576]{1,0:T(8,128)S(1)} %pad_maximum_fusion.11), channel_id=1, replica_groups=mesh['row'=16,'col'=8] {'col'}, dimensions={0}, use_global_device_ids=true | all-gather | bytes 165888 | tf_op jit(solution)/shard_map/all_gather | solution.py:22
  712.8 3.4 all-to-all-start.4
  717.2 26.9 %all-gather.11 = f32[16,144,64]{1,2,0:T(8,128)S(1)} all-gather(f32[1,144,64]{1,2,0:T(8,128)S(1)} %get-tuple-element.80), channel_id=6, replica_groups=mesh['row'=16,'col'=8] {'row'}, dimensions={0}, use_global_device_ids=true | all-gather | bytes 626688 | tf_op jit(solution)/shard_map/all_gather | solution.py:46
  749.6 22.4 %all_gather.100 = bf16[16,2,192,64]{2,3,1,0:T(8,128)(2,1)S(1)} all-gather(bf16[1,2,192,64]{2,3,1,0:T(8,128)(2,1)S(1)} %slice_bitcast_fusion.5), channel_id=1, replica_groups=mesh['row'=16,'col'=8] {'row'}, dimensions={0}, use_global_device_ids=true | all-gather | bytes 835584 | tf_op jit(solution)/shard_map/all_gather | solution.py:46
  778.3 5.2 all-to-all-start.5
  806.2 35.0 %reduce-scatter.8.cloned.1.call-done = f32[2028,8]{0,1:T(8,128)} async-done(((f32[2028,64]{0,1:T(8,128)}), f32[2028,8]{0,1:T(8,128)}) %reduce-scatter.8.cloned.1.call-update) | async-done | bytes 64912 | tf_op jit(solution)/shard_map/reduce_scatter | solution.py:55
  (544 shorter events, 154.3 us)
Async XLA Ops:
  7.2 497.7 %copy-start = (f32[2112,384]{1,0:T(8,128)S(1)}, f32[2112,384]{1,0:T(8,128)}, u32[]{:S(2)}) copy-start(f32[2112,384]{1,0:T(8,128)} %param.28) | copy-start | bytes 9732100
  7.2 44.7 %copy-start.105 = (s32[8]{0:T(128)S(1)}, s32[8]{0:T(128)}, u32[]{:S(2)}) copy-start(s32[8]{0:T(128)} %param.24) | copy-start | bytes 100
  10.1 402.7 %all-to-all-start = ((bf16[8,3,192,8]{2,3,1,0:T(8,128)(2,1)}), bf16[8,3,192,8]{2,3,1,0:T(8,128)(2,1)S(1)}, u32[]{:S(2)}, u32[]{:S(2)}) async-start(bf16[8,3,192,8]{2,3,1,0:T(8,128)(2,1)} %broadcast_in_dim.51), calls=%async_computation | async-start | bytes 196608 | tf_op jit(solution)/shard_map/all_to_all | solution.py:38
  15.6 445.1 %all-gather.17.cloned.1.call-start = ((), (), s32[]{:S(2)}) async-start(), calls=%async_computation.12 | async-start | bytes 1671168 | tf_op jit(solution)/shard_map/all_gather | solution.py:46
  19.2 348.8 %copy-start.28 = (bf16[128,128]{1,0:T(8,128)(2,1)S(1)}, bf16[128,128]{1,0:T(8,128)(2,1)}, u32[]{:S(2)}) copy-start(bf16[128,128]{1,0:T(8,128)(2,1)} %param.17) | copy-start | bytes 98308
  443.1 9.5 %all-to-all-start.1 = ((f32[8,1,768]{2,1,0:T(1,128)}), f32[8,1,768]{2,1,0:T(1,128)S(1)}, u32[]{:S(2)}, u32[]{:S(2)}) async-start(f32[8,1,768]{2,1,0:T(1,128)} %reshape.2142), calls=%async_computation.1 | async-start | bytes 49152 | tf_op jit(solution)/shard_map/all_to_all | solution.py:38
  446.4 54.1 %reduce-scatter.4.cloned.1.call-start = ((), (), s32[]{:S(2)}) async-start(), calls=%async_computation.9 | async-start | bytes 589824 | tf_op jit(solution)/shard_map/reduce_scatter | solution.py:55
  541.7 36.8 %all-to-all-start.2 = ((bf16[8,3,192,8]{2,3,1,0:T(8,128)(2,1)}), bf16[8,3,192,8]{2,3,1,0:T(8,128)(2,1)S(1)}, u32[]{:S(2)}, u32[]{:S(2)}) async-start(bf16[8,3,192,8]{2,3,1,0:T(8,128)(2,1)} %broadcast_in_dim.54), calls=%async_computation.3 | async-start | bytes 196608 | tf_op jit(solution)/shard_map/all_to_all | solution.py:38
  545.1 83.3 %all-gather.19.cloned.1.call-start = ((), (), s32[]{:S(2)}) async-start(), calls=%async_computation.13 | async-start | bytes 1671168 | tf_op jit(solution)/shard_map/all_gather | solution.py:46
  546.1 55.5 %copy-start.15 = (f32[144,64]{1,0:T(8,128)}, f32[144,64]{1,0:T(8,128)S(1)}, u32[]{:S(2)}) copy-start(f32[144,64]{1,0:T(8,128)S(1)} %copy.402) | copy-start | bytes 110596
  607.2 11.5 %all-to-all-start.3 = ((f32[8,1,768]{2,1,0:T(1,128)}), f32[8,1,768]{2,1,0:T(1,128)S(1)}, u32[]{:S(2)}, u32[]{:S(2)}) async-start(f32[8,1,768]{2,1,0:T(1,128)} %reshape.2144), calls=%async_computation.4 | async-start | bytes 49152 | tf_op jit(solution)/shard_map/all_to_all | solution.py:38
  612.4 57.7 %reduce-scatter.6.cloned.1.call-start = ((), (), s32[]{:S(2)}) async-start(), calls=%async_computation.10 | async-start | bytes 589824 | tf_op jit(solution)/shard_map/reduce_scatter | solution.py:55
  681.4 68.1 %copy-start.41 = (f32[1,8]{1,0:T(1,128)}, f32[1,8]{1,0:T(1,128)S(1)}, u32[]{:S(2)}) copy-start(f32[1,8]{1,0:T(1,128)S(1)} %get-tuple-element.157) | copy-start | bytes 100
  681.5 68.0 %copy-start.47 = (f32[1,8]{1,0:T(1,128)}, f32[1,8]{1,0:T(1,128)S(1)}, u32[]{:S(2)}) copy-start(f32[1,8]{1,0:T(1,128)S(1)} %get-tuple-element.154) | copy-start | bytes 100
  681.5 68.0 %copy-start.49 = (f32[1,8]{1,0:T(1,128)}, f32[1,8]{1,0:T(1,128)S(1)}, u32[]{:S(2)}) copy-start(f32[1,8]{1,0:T(1,128)S(1)} %get-tuple-element.155) | copy-start | bytes 100
  681.5 68.0 %copy-start.51 = (f32[1,8]{1,0:T(1,128)}, f32[1,8]{1,0:T(1,128)S(1)}, u32[]{:S(2)}) copy-start(f32[1,8]{1,0:T(1,128)S(1)} %get-tuple-element.156) | copy-start | bytes 100
  712.8 36.7 %all-to-all-start.4 = ((bf16[8,3,192,8]{2,3,1,0:T(8,128)(2,1)}), bf16[8,3,192,8]{2,3,1,0:T(8,128)(2,1)S(1)}, u32[]{:S(2)}, u32[]{:S(2)}) async-start(bf16[8,3,192,8]{2,3,1,0:T(8,128)(2,1)} %broadcast_in_dim.56), calls=%async_computation.6 | async-start | bytes 196608 | tf_op jit(solution)/shard_map/all_to_all | solution.py:38
  716.2 83.2 %all-gather.21.cloned.1.call-start = ((), (), s32[]{:S(2)}) async-start(), calls=%async_computation.14 | async-start | bytes 1671168 | tf_op jit(solution)/shard_map/all_gather | solution.py:46
  717.2 55.5 %copy-start.14 = (f32[144,64]{1,0:T(8,128)}, f32[144,64]{1,0:T(8,128)S(1)}, u32[]{:S(2)}) copy-start(f32[144,64]{1,0:T(8,128)S(1)} %copy.427) | copy-start | bytes 110596
  778.3 11.4 %all-to-all-start.5 = ((f32[8,1,768]{2,1,0:T(1,128)}), f32[8,1,768]{2,1,0:T(1,128)S(1)}, u32[]{:S(2)}, u32[]{:S(2)}) async-start(f32[8,1,768]{2,1,0:T(1,128)} %reshape.2146), calls=%async_computation.7 | async-start | bytes 49152 | tf_op jit(solution)/shard_map/all_to_all | solution.py:38
  783.5 57.7 %reduce-scatter.8.cloned.1.call-start = ((), (), s32[]{:S(2)}) async-start(), calls=%async_computation.11 | async-start | bytes 589824 | tf_op jit(solution)/shard_map/reduce_scatter | solution.py:55
  806.1 44.8 %copy-start.48 = (f32[1,8]{1,0:T(1,128)S(1)}, f32[1,8]{1,0:T(1,128)}, u32[]{:S(2)}) copy-start(f32[1,8]{1,0:T(1,128)} %copy-done.47) | copy-start | bytes 100
  806.1 44.8 %copy-start.50 = (f32[1,8]{1,0:T(1,128)S(1)}, f32[1,8]{1,0:T(1,128)}, u32[]{:S(2)}) copy-start(f32[1,8]{1,0:T(1,128)} %copy-done.49) | copy-start | bytes 100
  806.1 44.8 %copy-start.52 = (f32[1,8]{1,0:T(1,128)S(1)}, f32[1,8]{1,0:T(1,128)}, u32[]{:S(2)}) copy-start(f32[1,8]{1,0:T(1,128)} %copy-done.51) | copy-start | bytes 100
  (96 other events, 1063.7 us)
Sparse Core Ops, SparseCore 0:
  51.3 47.5 all-gather.16
  467.7 32.7 reduce-scatter.3
  576.4 43.9 all-gather.18
  635.2 34.8 reduce-scatter.5
  747.4 44.0 all-gather.20
  806.2 34.8 reduce-scatter.7
where the time goes:
time: 863 us; the launch traced here: 859 us
  blocking collectives  543 us (63%)
  waiting for transfers between devices  111 us (13%)
  local copies, waits for them, and re-layouts  74.6 us (9%)
  matrix products  52.3 us (6%)
  other arithmetic  35.2 us (4%)
  starting transfers between devices  26.8 us (3%)
  between operations  16.3 us (2%)
    all_gather x4, blocking collectives, rows_first(): whole, at, outs = (lax.all_gather(both, axis, axis=0, tiled=True), 0, [])  397 us
    all_gather x6, blocking collectives, broadcast(): lax.all_gather(value, axis)  146 us
    reduce_scatter x3, waiting for transfers between devices, sent_together(): lax.psum_scatter(both, axis, scatter_dimension=dim, tiled=True)  103 us
    unnamed x246, local copies, waits for them, and re-layouts  31.3 us
    all_to_all x6, starting transfers between devices, copy_for_each(): return lax.all_to_all(copies, axis, split_axis=0, concat_axis=0, tiled=True)  25.9 us
  transfers between devices with their start and end apart: 12, of which 6 were waited for; matrix products, arithmetic and copies ran while one was open for 11% of the time, Pallas kernels for 0%

commit v1 on v0

--- a/solution.py
+++ b/solution.py
@@ -16,10 +16,15 @@
 HIGHEST_PRECISION = lax.Precision.HIGHEST
 
 
+def all_by_exchange(x, name, d):
+    sent = jnp.stack([x] * lax.axis_size(name))
+    return jnp.concatenate(lax.all_to_all(sent, name, 0, 0), axis=d)
+
+
 def rows_first(arrays, axis, dims):
     turned = [jnp.moveaxis(a, dim, 0) for a, dim in zip(arrays, dims)]
     both = jnp.concatenate([t.reshape(len(t), -1) for t in turned], axis=1)
-    whole, at, outs = (lax.all_gather(both, axis, axis=0, tiled=True), 0, [])
+    whole, at, outs = (all_by_exchange(both, axis, 0), 0, [])
     for t, dim in zip(turned, dims):
         piece = whole[:, at : at + t[0].size].reshape(-1, *t.shape[1:])
         outs.append(jnp.moveaxis(piece, 0, dim))

time: 863 us -> 495 us (0.57)
  blocking collectives: 543 us -> 149 us
  starting transfers between devices: 26.8 us -> 52.2 us
  waiting for transfers between devices: 111 us -> 129 us
  local copies, waits for them, and re-layouts: 74.6 us -> 65 us
    all_gather x4 -> x0, blocking collectives: 397 us -> none  [rows_first(): whole, at, outs = (lax.all_gather(both, axis, axis=0, tiled=True), 0, [])]
    all_to_all x0 -> x4, starting transfers between devices: none -> 23.7 us  [all_by_exchange(): return jnp.concatenate(lax.all_to_all(sent, name, 0, 0), axis=d)]
    all_to_all x6, waiting for transfers between devices: 7.99 us -> 24.7 us  [copy_for_each(): return lax.all_to_all(copies, axis, split_axis=0, concat_axis=0, tiled=True)]
    unnamed x246 -> x223, local copies, waits for them, and re-layouts: 31.3 us -> 20.4 us
  transfers between devices with their start and end apart: 12 -> 16, of which waited for: 6 -> 8; matrix products, arithmetic and copies ran while one was open for 11% -> 17% of each run, Pallas kernels for 0% -> 0%
where the time goes in v1:
time: 495 us; the launch traced here: 492 us
  blocking collectives  149 us (30%)
  waiting for transfers between devices  129 us (26%)
  local copies, waits for them, and re-layouts  65 us (13%)
  matrix products  54.6 us (11%)
  starting transfers between devices  52.2 us (11%)
  other arithmetic  26.7 us (5%)
  between operations  16.2 us (3%)
    all_gather x6, blocking collectives, broadcast(): lax.all_gather(value, axis)  149 us
    reduce_scatter x3, waiting for transfers between devices, sent_together(): lax.psum_scatter(both, axis, scatter_dimension=dim, tiled=True)  104 us
    all_to_all x6, starting transfers between devices, copy_for_each(): return lax.all_to_all(copies, axis, split_axis=0, concat_axis=0, tiled=True)  27.7 us
    all_to_all x6, waiting for transfers between devices, copy_for_each(): return lax.all_to_all(copies, axis, split_axis=0, concat_axis=0, tiled=True)  24.7 us
    all_to_all x4, starting transfers between devices, all_by_exchange(): return jnp.concatenate(lax.all_to_all(sent, name, 0, 0), axis=d)  23.7 us
    unnamed x223, local copies, waits for them, and re-layouts  20.4 us
  transfers between devices with their start and end apart: 16, of which 8 were waited for; matrix products, arithmetic and copies ran while one was open for 17% of the time, Pallas kernels for 0%

profile of v1, /device:TPU:0, one launch (start us, length us, event | category | flops | bytes accessed | tf_op | source)
XLA Modules:
  0.0 492.1 jit_solution(3099421878493681701)
XLA Ops:
  8.7 11.2 %all-to-all-start = ((s32[128,8,2]{1,2,0:T(2,128)}), s32[128,8,2]{1,2,0:T(2,128)S(1)}, u32[]{:S(2)}, u32[]{:S(2)}) async-start(s32[128,8,2]{1,2,0:T(2,128)} %stack.94), calls=%async_computation | async-start | bytes 262144 | tf_op jit(solution)/shard_map/all_to_all | solution.py:21
  29.5 4.1 copy.359
  34.2 4.6 all-to-all-start.1
  39.3 3.8 fusion.95
  48.1 5.7 %all-to-all-start.2 = ((f32[8,8,576]{2,1,0:T(8,128)}), f32[8,8,576]{2,1,0:T(8,128)S(1)}, u32[]{:S(2)}, u32[]{:S(2)}) async-start(f32[8,8,576]{2,1,0:T(8,128)} %stack.108), calls=%async_computation.2 | async-start | bytes 327680 | tf_op jit(solution)/shard_map/all_to_all | solution.py:21
  54.8 27.5 %all_gather.73 = bf16[16,2,192,64]{2,3,1,0:T(8,128)(2,1)S(1)} all-gather(bf16[1,2,192,64]{2,3,1,0:T(8,128)(2,1)S(1)} %slice_bitcast_fusion.11), channel_id=1, replica_groups=mesh['row'=16,'col'=8] {'row'}, dimensions={0}, use_global_device_ids=true | all-gather | bytes 835584 | tf_op jit(solution)/shard_map/all_gather | solution.py:51
  89.1 22.4 %all-gather.6 = f32[16,144,64]{1,2,0:T(8,128)S(1)} all-gather(f32[1,144,64]{1,2,0:T(8,128)S(1)} %get-tuple-element.84), channel_id=2, replica_groups=mesh['row'=16,'col'=8] {'row'}, dimensions={0}, use_global_device_ids=true | all-gather | bytes 626688 | tf_op jit(solution)/shard_map/all_gather | solution.py:51
  115.3 5.6 %all-to-all-start.3 = ((f32[8,1,768]{2,1,0:T(1,128)}), f32[8,1,768]{2,1,0:T(1,128)S(1)}, u32[]{:S(2)}, u32[]{:S(2)}) async-start(f32[8,1,768]{2,1,0:T(1,128)} %reshape.2164), calls=%async_computation.3 | async-start | bytes 49152 | tf_op jit(solution)/shard_map/all_to_all | solution.py:43
  122.4 4.7 all-to-all-done.3
  142.1 34.6 %reduce-scatter.4.cloned.1.call-done = f32[2028,8]{0,1:T(8,128)} async-done(((f32[2028,64]{0,1:T(8,128)}), f32[2028,8]{0,1:T(8,128)}) %reduce-scatter.4.cloned.1.call-update) | async-done | bytes 64912 | tf_op jit(solution)/shard_map/reduce_scatter | solution.py:60
  191.6 6.0 %all-to-all-done.4 = bf16[8,3,192,8]{2,3,1,0:T(8,128)(2,1)S(1)} async-done(((bf16[8,3,192,8]{2,3,1,0:T(8,128)(2,1)}), bf16[8,3,192,8]{2,3,1,0:T(8,128)(2,1)S(1)}, u32[]{:S(2)}, u32[]{:S(2)}) %all-to-all-start.4) | async-done | bytes 73760 | tf_op jit(solution)/shard_map/all_to_all | solution.py:43
  198.3 3.4 all-to-all-start.5
  201.8 27.0 %all_gather.79 = bf16[16,2,192,64]{2,3,1,0:T(8,128)(2,1)S(1)} all-gather(bf16[1,2,192,64]{2,3,1,0:T(8,128)(2,1)S(1)} %slice_bitcast_fusion.8), channel_id=1, replica_groups=mesh['row'=16,'col'=8] {'row'}, dimensions={0}, use_global_device_ids=true | all-gather | bytes 835584 | tf_op jit(solution)/shard_map/all_gather | solution.py:51
  235.6 22.4 %all-gather.8 = f32[16,144,64]{1,2,0:T(8,128)S(1)} all-gather(f32[1,144,64]{1,2,0:T(8,128)S(1)} %get-tuple-element.82), channel_id=4, replica_groups=mesh['row'=16,'col'=8] {'row'}, dimensions={0}, use_global_device_ids=true | all-gather | bytes 626688 | tf_op jit(solution)/shard_map/all_gather | solution.py:51
  261.8 5.5 %all-to-all-start.6 = ((f32[8,1,768]{2,1,0:T(1,128)}), f32[8,1,768]{2,1,0:T(1,128)S(1)}, u32[]{:S(2)}, u32[]{:S(2)}) async-start(f32[8,1,768]{2,1,0:T(1,128)} %reshape.2166), calls=%async_computation.7 | async-start | bytes 49152 | tf_op jit(solution)/shard_map/all_to_all | solution.py:43
  269.5 4.0 all-to-all-done.6
  290.0 34.5 %reduce-scatter.6.cloned.1.call-done = f32[2028,8]{0,1:T(8,128)} async-done(((f32[2028,64]{0,1:T(8,128)}), f32[2028,8]{0,1:T(8,128)}) %reduce-scatter.6.cloned.1.call-update) | async-done | bytes 64912 | tf_op jit(solution)/shard_map/reduce_scatter | solution.py:60
  340.9 6.0 %all-to-all-done.7 = bf16[8,3,192,8]{2,3,1,0:T(8,128)(2,1)S(1)} async-done(((bf16[8,3,192,8]{2,3,1,0:T(8,128)(2,1)}), bf16[8,3,192,8]{2,3,1,0:T(8,128)(2,1)S(1)}, u32[]{:S(2)}, u32[]{:S(2)}) %all-to-all-start.7) | async-done | bytes 73760 | tf_op jit(solution)/shard_map/all_to_all | solution.py:43
  347.7 3.4 all-to-all-start.8
  351.1 27.0 %all_gather.85 = bf16[16,2,192,64]{2,3,1,0:T(8,128)(2,1)S(1)} all-gather(bf16[1,2,192,64]{2,3,1,0:T(8,128)(2,1)S(1)} %slice_bitcast_fusion.5), channel_id=1, replica_groups=mesh['row'=16,'col'=8] {'row'}, dimensions={0}, use_global_device_ids=true | all-gather | bytes 835584 | tf_op jit(solution)/shard_map/all_gather | solution.py:51
  384.9 22.4 %all-gather.10 = f32[16,144,64]{1,2,0:T(8,128)S(1)} all-gather(f32[1,144,64]{1,2,0:T(8,128)S(1)} %get-tuple-element.80), channel_id=6, replica_groups=mesh['row'=16,'col'=8] {'row'}, dimensions={0}, use_global_device_ids=true | all-gather | bytes 626688 | tf_op jit(solution)/shard_map/all_gather | solution.py:51
  411.0 5.2 %all-to-all-start.9 = ((f32[8,1,768]{2,1,0:T(1,128)}), f32[8,1,768]{2,1,0:T(1,128)S(1)}, u32[]{:S(2)}, u32[]{:S(2)}) async-start(f32[8,1,768]{2,1,0:T(1,128)} %reshape.2168), calls=%async_computation.11 | async-start | bytes 49152 | tf_op jit(solution)/shard_map/all_to_all | solution.py:43
  418.5 4.0 all-to-all-done.9
  438.9 35.0 %reduce-scatter.8.cloned.1.call-done = f32[2028,8]{0,1:T(8,128)} async-done(((f32[2028,64]{0,1:T(8,128)}), f32[2028,8]{0,1:T(8,128)}) %reduce-scatter.8.cloned.1.call-update) | async-done | bytes 64912 | tf_op jit(solution)/shard_map/reduce_scatter | solution.py:60
  (530 shorter events, 146.1 us)
Async XLA Ops:
  7.2 173.9 %copy-start = (f32[2112,384]{1,0:T(8,128)S(1)}, f32[2112,384]{1,0:T(8,128)}, u32[]{:S(2)}) copy-start(f32[2112,384]{1,0:T(8,128)} %param.28) | copy-start | bytes 9732100
  8.7 24.9 %all-to-all-start = ((s32[128,8,2]{1,2,0:T(2,128)}), s32[128,8,2]{1,2,0:T(2,128)S(1)}, u32[]{:S(2)}, u32[]{:S(2)}) async-start(s32[128,8,2]{1,2,0:T(2,128)} %stack.94), calls=%async_computation | async-start | bytes 262144 | tf_op jit(solution)/shard_map/all_to_all | solution.py:21
  34.2 13.2 %all-to-all-start.1 = ((bf16[8,3,192,8]{2,3,1,0:T(8,128)(2,1)}), bf16[8,3,192,8]{2,3,1,0:T(8,128)(2,1)}, u32[]{:S(2)}, u32[]{:S(2)}) async-start(bf16[8,3,192,8]{2,3,1,0:T(8,128)(2,1)} %broadcast_in_dim.51), calls=%async_computation.1 | async-start | bytes 196608 | tf_op jit(solution)/shard_map/all_to_all | solution.py:43
  47.4 64.4 %copy-start.89 = (pred[64,128]{1,0:T(8,128)(4,1)}, pred[64,128]{1,0:T(8,128)(4,1)S(1)}, u32[]{:S(2)}) copy-start(pred[64,128]{1,0:T(8,128)(4,1)S(1)} %broadcast_and_fusion) | copy-start | bytes 24580
  48.1 37.9 %all-to-all-start.2 = ((f32[8,8,576]{2,1,0:T(8,128)}), f32[8,8,576]{2,1,0:T(8,128)S(1)}, u32[]{:S(2)}, u32[]{:S(2)}) async-start(f32[8,8,576]{2,1,0:T(8,128)} %stack.108), calls=%async_computation.2 | async-start | bytes 327680 | tf_op jit(solution)/shard_map/all_to_all | solution.py:21
  53.8 81.4 %all-gather.16.cloned.1.call-start = ((), (), s32[]{:S(2)}) async-start(), calls=%async_computation.16 | async-start | bytes 1671168 | tf_op jit(solution)/shard_map/all_gather | solution.py:51
  115.3 11.8 %all-to-all-start.3 = ((f32[8,1,768]{2,1,0:T(1,128)}), f32[8,1,768]{2,1,0:T(1,128)S(1)}, u32[]{:S(2)}, u32[]{:S(2)}) async-start(f32[8,1,768]{2,1,0:T(1,128)} %reshape.2164), calls=%async_computation.3 | async-start | bytes 49152 | tf_op jit(solution)/shard_map/all_to_all | solution.py:43
  120.8 55.9 %reduce-scatter.4.cloned.1.call-start = ((), (), s32[]{:S(2)}) async-start(), calls=%async_computation.13 | async-start | bytes 589824 | tf_op jit(solution)/shard_map/reduce_scatter | solution.py:60
  139.8 39.2 %copy-start.66 = (f32[8]{0:T(128)S(1)}, f32[8]{0:T(128)}, u32[]{:S(2)}) copy-start(f32[8]{0:T(128)} %copy-done.65) | copy-start | bytes 100
  139.9 41.2 %copy-start.16 = (f32[8,384]{1,0:T(8,128)S(1)}, f32[8,384]{1,0:T(8,128)}, u32[]{:S(2)}) copy-start(f32[8,384]{1,0:T(8,128)} %param.20) | copy-start | bytes 36868
  186.5 43.0 %copy-start.22 = (f32[1,8]{1,0:T(1,128)}, f32[1,8]{1,0:T(1,128)S(1)}, u32[]{:S(2)}) copy-start(f32[1,8]{1,0:T(1,128)S(1)} %get-tuple-element.119) | copy-start | bytes 100
  187.9 9.7 %all-to-all-start.4 = ((bf16[8,3,192,8]{2,3,1,0:T(8,128)(2,1)}), bf16[8,3,192,8]{2,3,1,0:T(8,128)(2,1)S(1)}, u32[]{:S(2)}, u32[]{:S(2)}) async-start(bf16[8,3,192,8]{2,3,1,0:T(8,128)(2,1)} %broadcast_in_dim.54), calls=%async_computation.5 | async-start | bytes 196608 | tf_op jit(solution)/shard_map/all_to_all | solution.py:43
  198.3 34.3 %all-to-all-start.5 = ((f32[8,8,576]{2,1,0:T(8,128)}), f32[8,8,576]{2,1,0:T(8,128)S(1)}, u32[]{:S(2)}, u32[]{:S(2)}) async-start(f32[8,8,576]{2,1,0:T(8,128)} %stack.123), calls=%async_computation.6 | async-start | bytes 327680 | tf_op jit(solution)/shard_map/all_to_all | solution.py:21
  201.7 81.5 %all-gather.18.cloned.1.call-start = ((), (), s32[]{:S(2)}) async-start(), calls=%async_computation.17 | async-start | bytes 1671168 | tf_op jit(solution)/shard_map/all_gather | solution.py:51
  261.8 11.7 %all-to-all-start.6 = ((f32[8,1,768]{2,1,0:T(1,128)}), f32[8,1,768]{2,1,0:T(1,128)S(1)}, u32[]{:S(2)}, u32[]{:S(2)}) async-start(f32[8,1,768]{2,1,0:T(1,128)} %reshape.2166), calls=%async_computation.7 | async-start | bytes 49152 | tf_op jit(solution)/shard_map/all_to_all | solution.py:43
  267.3 57.2 %reduce-scatter.6.cloned.1.call-start = ((), (), s32[]{:S(2)}) async-start(), calls=%async_computation.14 | async-start | bytes 589824 | tf_op jit(solution)/shard_map/reduce_scatter | solution.py:60
  337.2 9.7 %all-to-all-start.7 = ((bf16[8,3,192,8]{2,3,1,0:T(8,128)(2,1)}), bf16[8,3,192,8]{2,3,1,0:T(8,128)(2,1)S(1)}, u32[]{:S(2)}, u32[]{:S(2)}) async-start(bf16[8,3,192,8]{2,3,1,0:T(8,128)(2,1)} %broadcast_in_dim.56), calls=%async_computation.9 | async-start | bytes 196608 | tf_op jit(solution)/shard_map/all_to_all | solution.py:43
  347.7 34.2 %all-to-all-start.8 = ((f32[8,8,576]{2,1,0:T(8,128)}), f32[8,8,576]{2,1,0:T(8,128)S(1)}, u32[]{:S(2)}, u32[]{:S(2)}) async-start(f32[8,8,576]{2,1,0:T(8,128)} %stack.138), calls=%async_computation.10 | async-start | bytes 327680 | tf_op jit(solution)/shard_map/all_to_all | solution.py:21
  351.1 81.1 %all-gather.20.cloned.1.call-start = ((), (), s32[]{:S(2)}) async-start(), calls=%async_computation.18 | async-start | bytes 1671168 | tf_op jit(solution)/shard_map/all_gather | solution.py:51
  411.0 11.5 %all-to-all-start.9 = ((f32[8,1,768]{2,1,0:T(1,128)}), f32[8,1,768]{2,1,0:T(1,128)S(1)}, u32[]{:S(2)}, u32[]{:S(2)}) async-start(f32[8,1,768]{2,1,0:T(1,128)} %reshape.2168), calls=%async_computation.11 | async-start | bytes 49152 | tf_op jit(solution)/shard_map/all_to_all | solution.py:43
  416.3 57.6 %reduce-scatter.8.cloned.1.call-start = ((), (), s32[]{:S(2)}) async-start(), calls=%async_computation.15 | async-start | bytes 589824 | tf_op jit(solution)/shard_map/reduce_scatter | solution.py:60
  438.9 44.7 %copy-start.39 = (f32[1,8]{1,0:T(1,128)S(1)}, f32[1,8]{1,0:T(1,128)}, u32[]{:S(2)}) copy-start(f32[1,8]{1,0:T(1,128)} %copy-done.38) | copy-start | bytes 100
  438.9 44.7 %copy-start.41 = (f32[1,8]{1,0:T(1,128)S(1)}, f32[1,8]{1,0:T(1,128)}, u32[]{:S(2)}) copy-start(f32[1,8]{1,0:T(1,128)} %copy-done.40) | copy-start | bytes 100
  438.9 44.7 %copy-start.43 = (f32[1,8]{1,0:T(1,128)S(1)}, f32[1,8]{1,0:T(1,128)}, u32[]{:S(2)}) copy-start(f32[1,8]{1,0:T(1,128)} %copy-done.42) | copy-start | bytes 100
  (89 other events, 853.4 us)
Sparse Core Ops, SparseCore 0:
  86.9 44.2 all-gather.15
  142.3 34.4 reduce-scatter.3
  233.5 44.0 all-gather.17
  290.1 34.3 reduce-scatter.5
  382.7 44.0 all-gather.19
  439.0 34.8 reduce-scatter.7
